TPU v7x, 32 devices: a whole 2x2x4 slice. The times are simulated.
32 devices in a mesh: pb: 4 (over y, x), wa: 8 (over z, core).
Axes of the slice: x: 2, y: 2, z: 4, core: 2. Of those that a mesh axis runs over, the one named last changes fastest.
Arguments:
- quartets: int32 [1024, 4, 128], P(('pb', 'wa')), may hold values from -1 to 49151, as said below
- counts: int32 [32], P(('pb', 'wa')), may hold values from 1 to 32, as said below
- eig: bfloat16 [24, 49152], P(None, 'pb'), may hold values from -1.1953125 to 1.1953125
- freq: bfloat16 [49152], P('pb'), may hold values from 0.5 to 2
- phi: bfloat16 [144, 1152], replicated, may hold values from -0.5390625 to 0.5390625
- cells: int32 [8, 9], replicated, may hold values from -2 to 2
Outputs:
- rates: float32 [49152], P(('pb', 'wa'))
Inputs may be any that keep to these rules, and one draw needn't show every extreme that they name: quartets[b, 0, n] is a mode of one of the 1024 q-points of the owner group of slot b (from 0 to 12287); the other three entries are all -1 or all modes of the mesh, and then their q-points and that of the first add up as q1 + q2 = q3 + q4 on the mesh. The used slots of a device are its first counts slots; some device has exactly 32.
All inputs are finite; a program needn't handle non-finite values.
Results may differ from a plain program's by a relative error of at most 0.0023.
Values may be sent and summed in bfloat16 or wider, within the bound.
A program may use at most 64 MiB of HBM per device.

v0:
```python
import math
import jax
import jax.numpy as jnp
from jax import lax
from jax.sharding import PartitionSpec as P

QMESH = 16
smearing = 0.5


def outer_pair(first, second, branches):
    count = first.shape[1]
    first_re = first[:branches][:, None, :]
    first_im = first[branches:][:, None, :]
    second_re = second[:branches][None, :, :]
    second_im = second[branches:][None, :, :]
    real = (first_re * second_re - first_im * second_im).reshape(branches * branches, count)
    imag = (first_re * second_im + first_im * second_re).reshape(branches * branches, count)
    return (real, imag)


def cluster_phase(other_modes, cells, branches):
    points = other_modes // branches
    coords = [points // (QMESH * QMESH), points // QMESH % QMESH, points % QMESH]
    shift = jnp.zeros((cells.shape[0], other_modes.shape[1]), jnp.int32)
    for which in range(3):
        sign = 1 if which == 0 else -1
        for axis_c in range(3):
            shift = (
                shift
                + sign * cells[:, 3 * which + axis_c][:, None] * coords[axis_c][which][None, :]
            )
    angle = jnp.remainder(shift, QMESH).astype(jnp.float32) * (2.0 * math.pi / QMESH)
    return (jnp.cos(angle), jnp.sin(angle))


def occupation(value):
    return 1.0 / (jnp.exp(value) - 1.0)


def contributions(
    first_modes,
    other_modes,
    other_spots,
    valid,
    first_vectors,
    first_freqs,
    vectors,
    frequencies,
    phi,
    cells,
):
    branches = vectors.shape[0] // 2
    count = first_modes.shape[0]
    clusters = cells.shape[0]
    first_vec = jnp.take(first_vectors, first_modes, axis=1).astype(jnp.float32)
    first_freq = jnp.take(first_freqs, first_modes).astype(jnp.float32)
    flat_spots = other_spots.reshape(3 * count)
    gathered = jnp.take(vectors, flat_spots, axis=1).astype(jnp.float32)
    other_freq = jnp.take(frequencies, flat_spots).astype(jnp.float32).reshape(3, count)
    second_vec = gathered[:, :count]
    third_vec = gathered[:, count : 2 * count]
    fourth_vec = gathered[:, 2 * count :]
    far_re, far_im = outer_pair(third_vec, fourth_vec, branches)
    far_im = -far_im
    cosine, sine = cluster_phase(other_modes, cells, branches)
    wide_re = cosine[:, None, :] * far_re[None] - sine[:, None, :] * far_im[None]
    wide_im = cosine[:, None, :] * far_im[None] + sine[:, None, :] * far_re[None]
    wide_re = wide_re.reshape(clusters * branches * branches, count).astype(jnp.bfloat16)
    wide_im = wide_im.reshape(clusters * branches * branches, count).astype(jnp.bfloat16)
    weighted_re = jnp.dot(phi, wide_re, preferred_element_type=jnp.float32)
    weighted_im = jnp.dot(phi, wide_im, preferred_element_type=jnp.float32)
    near_re, near_im = outer_pair(first_vec, second_vec, branches)
    value_re = jnp.sum(near_re * weighted_re - near_im * weighted_im, axis=0)
    value_im = jnp.sum(near_re * weighted_im + near_im * weighted_re, axis=0)
    mismatch = first_freq + other_freq[0] - other_freq[1] - other_freq[2]
    delta = jnp.exp(-((mismatch / smearing) ** 2)) / (smearing * math.sqrt(math.pi))
    weight = (
        (1.0 + occupation(other_freq[0]))
        * occupation(other_freq[1])
        * occupation(other_freq[2])
        / occupation(first_freq)
    )
    product = first_freq * other_freq[0] * other_freq[1] * other_freq[2]
    return jnp.where(
        valid, (value_re * value_re + value_im * value_im) * delta * weight / product, 0.0
    )


def body(quartets, counts, eig, freq, phi, cells):
    local_modes = eig.shape[1]
    workers = lax.axis_size("wa")
    held = quartets.shape[0]
    block = quartets.shape[2]
    group = math.gcd(held, 16)
    table, freq_table = (
        lax.all_gather(eig, "pb", axis=1, tiled=True),
        lax.all_gather(freq, "pb", axis=0, tiled=True),
    )
    per_dest = held // workers
    dealt = quartets.reshape(per_dest, workers, 4, block)
    tallies = jnp.full((1, workers), counts[0], jnp.int32)
    dealt, tallies = (
        lax.all_to_all(dealt, "wa", split_axis=1, concat_axis=1, tiled=True),
        lax.all_to_all(tallies, "wa", split_axis=1, concat_axis=1, tiled=True),
    )
    slot_index = jnp.arange(per_dest, dtype=jnp.int32)[:, None] * workers + lax.axis_index("wa")
    used = (slot_index < tallies).reshape(held)
    pool = dealt.reshape(held, 4, block)
    rank = jnp.cumsum(used.astype(jnp.int32)) - 1
    target = jnp.where(used, rank, held)
    order = (
        jnp.zeros((held,), jnp.int32).at[target].set(jnp.arange(held, dtype=jnp.int32), mode="drop")
    )
    total = jnp.sum(used.astype(jnp.int32))

    def fetch(start):
        picks = lax.dynamic_slice_in_dim(order, start, group, 0)
        return jnp.take(pool, picks, axis=0)

    rounds = (total + group - 1) // group

    def one_round(step, partial_value):
        start = (step * group).astype(jnp.int32)
        blocks = fetch(start)
        live = start + jnp.arange(group, dtype=jnp.int32) < total
        first_modes = blocks[:, 0, :].reshape(group * block)
        others = jnp.transpose(blocks[:, 1:, :], (1, 0, 2)).reshape(3, group * block)
        valid = (others[0] >= 0) & jnp.repeat(live, block)
        clamped = jnp.maximum(others, 0)
        terms = contributions(
            first_modes, clamped, clamped, valid, eig, freq, table, freq_table, phi, cells
        )
        return partial_value.at[first_modes].add(terms)

    partial_value = lax.fori_loop(0, rounds, one_round, jnp.zeros((local_modes,), jnp.float32))
    return lax.psum_scatter(partial_value, "wa", scatter_dimension=0, tiled=True)


def solution(mesh):
    placed = (P(("pb", "wa"), None, None), P(("pb", "wa")), P(None, "pb"), P("pb"), P(), P())
    return jax.shard_map(
        body, mesh=mesh, in_specs=placed, out_specs=P(("pb", "wa")), check_vma=False
    )
```

profile of v0, /device:TPU:4, one launch (start us, length us, event | category | flops | bytes accessed | tf_op | source)
XLA Modules:
  0.0 432.6 jit_solution(528731850995991706)
XLA Ops:
  6.5 3.7 copy.98
  11.6 4.9 %all-to-all-start = ((s32[1,8,1]{2,0,1:T(1,128)}), s32[1,8,1]{2,0,1:T(1,128)S(1)}, u32[]{:S(2)}, u32[]{:S(2)}) async-start(s32[1,8,1]{2,0,1:T(1,128)} %broadcast_in_dim.123), calls=%async_computation | async-start | bytes 8192 | tf_op jit(solution)/shard_map/all_to_all | solution.py:105
  17.8 9.0 %all_gather.7 = bf16[49152]{0:T(1024)(128)(2,1)S(1)} all-gather(bf16[12288]{0:T(1024)(128)(2,1)S(1)} %copy-done), channel_id=1, replica_groups=mesh['pb'=4,'wa'=8] {'pb'}, dimensions={0}, use_global_device_ids=true | all-gather | bytes 122880 | tf_op jit(solution)/shard_map/all_gather | solution.py:98
  27.3 5.1 %all-to-all-start.1 = ((s32[4,8,4,128]{3,2,0,1:T(4,128)}), s32[4,8,4,128]{3,2,0,1:T(4,128)S(1)}, u32[]{:S(2)}, u32[]{:S(2)}) async-start(s32[4,8,4,128]{3,2,0,1:T(4,128)} %copy.94), calls=%async_computation.1 | async-start | bytes 131072 | tf_op jit(solution)/shard_map/all_to_all | solution.py:104
  35.2 3.2 all-to-all-done.1
  38.4 95.9 %all-gather.2.cloned.1.call-done = bf16[24,49152]{0,1:T(8,128)(2,1)} async-done(((bf16[24,12288]{0,1:T(8,128)(2,1)}), bf16[24,49152]{0,1:T(8,128)(2,1)}) %all-gather.2.cloned.1.call-update) | async-done | bytes 2359312 | tf_op jit(solution)/shard_map/all_gather | solution.py:97
  134.3 264.4 %while.13 = (s32[]{:T(128)}, f32[12288]{0:T(1024)S(1)}, s32[]{:T(128)}, s32[32]{0:T(128)S(1)}, s32[32,4,128]{2,1,0:T(4,128)S(1)}, /*index=5*/s32[]{:T(128)}, bf1...) while((s32[]{:T(128)}, f32[12288]{0:T(1024)S(1)}, ...), condition=%wide.region_7.8_spmd, body=%wide.region_3.7_spmd.sunk | while | flops 1385344256 | bytes 61334244 | solution.py:136
  136.3 22.7 %gather_fusion.2 = bf16[6144,24]{1,0:T(8,128)(2,1)S(1)} fusion(bf16[24,49152]{0,1:T(8,128)(2,1)} %get-tuple-element.560, s32[6144]{0:T(1024)S(1)} %broadcast_clamp_fusion.4), kind=kCustom, calls=%fused_computation.2.clone.1 | custom fusion | bytes 614400 | tf_op jit(solution)/shard_map/while/body/jit(_take)/gather | solution.py:59
  160.1 2.5 fusion.55
  171.6 5.2 %subtract_convert_fusion.2 = (bf16[8,144,2048]{2,1,0:T(8,128)(2,1)S(1)}, bf16[8,144,2048]{2,1,0:T(8,128)(2,1)}) fusion(f32[144,2048]{1,0:T(8,128)S(1)} %copy-done.1, f32[8,2048]{1,0:T(8,128)S(1)} %get-tuple-element.513, f32[144,2048]{1,0:T(8,128)} %sub.196, f32[8,2048]{1,0:T(8,128)S(1)} %get-tuple-element.515), kind=kLoop, calls=%fused_computation.8.clone.1 | loop fusion | flops 18874368 | bytes 11927552 | tf_op jit(solution)/shard_map/while/body/convert_element_type | solution.py:69
  181.0 7.9 %gather_fusion.3 = bf16[2048,24]{1,0:T(8,128)(2,1)S(1)} fusion(bf16[24,12288]{0,1:T(8,128)(2,1)} %get-tuple-element.559, s32[2048]{0:T(1024)S(1)} %broadcast_clamp_fusion.5), kind=kCustom, calls=%fused_computation.1.clone.1 | custom fusion | bytes 204800 | tf_op jit(solution)/shard_map/while/body/jit(_take)/gather | solution.py:56
  195.9 4.4 %subtract_reduce_fusion.2 = (f32[2048]{0:T(1024)S(1)}, f32[2048]{0:T(1024)S(1)}) fusion(f32[144,2048]{1,0:T(8,128)} %add.543, f32[144,2048]{1,0:T(8,128)} %sub.195, f32[144,2048]{1,0:T(8,128)S(1)} %copy-done.2, bf16[144,1152]{1,0:T(8,128)(2,1)S(1)} %copy-done.6, bf16[1152,2048]{1,0:T(8,128)(2,1)} %bitcast.164), kind=kOutput, calls=%fused_computation.17.clone.1 | convolution fusion | flops 681832448 | bytes 8605696 | tf_op jit(solution)/shard_map/while/body/dot_general | solution.py:72
  200.4 38.2 %gather_fusion.1 = bf16[6144]{0:T(1024)(128)(2,1)S(1)} fusion(bf16[49152]{0:T(1024)(128)(2,1)S(1)} %get-tuple-element.564, s32[6144]{0:T(1024)S(1)} %broadcast_clamp_fusion.4), kind=kCustom, calls=%fused_computation.4.clone.1 | custom fusion | bytes 49152 | tf_op jit(solution)/shard_map/while/body/jit(_take)/gather | solution.py:60
  238.6 13.1 %gather_fusion.4 = bf16[2048]{0:T(1024)(128)(2,1)S(1)} fusion(bf16[12288]{0:T(1024)(128)(2,1)S(1)} %get-tuple-element.563, s32[2048]{0:T(1024)S(1)} %broadcast_clamp_fusion.5), kind=kCustom, calls=%fused_computation.3.clone.1 | custom fusion | bytes 16384 | tf_op jit(solution)/shard_map/while/body/jit(_take)/gather | solution.py:57
  251.8 14.7 %scatter_fusion = f32[12288]{0:T(1024)S(1)} fusion(f32[12288]{0:T(1024)S(1)} %get-tuple-element.538, s32[2048]{0:T(1024)S(1)} %bitcast.168, f32[2048]{0:T(1024)S(1)} %fusion.61), kind=kCustom, calls=%fused_computation.5.clone.1 | custom fusion | flops 2048 | bytes 32768 | tf_op jit(solution)/shard_map/while/body/scatter-add | solution.py:134
  268.5 22.6 %gather_fusion.2 = bf16[6144,24]{1,0:T(8,128)(2,1)S(1)} fusion(bf16[24,49152]{0,1:T(8,128)(2,1)} %get-tuple-element.560, s32[6144]{0:T(1024)S(1)} %broadcast_clamp_fusion.4), kind=kCustom, calls=%fused_computation.2.clone.1 | custom fusion | bytes 614400 | tf_op jit(solution)/shard_map/while/body/jit(_take)/gather | solution.py:59
  292.3 2.5 fusion.55
  303.8 5.2 %subtract_convert_fusion.2 = (bf16[8,144,2048]{2,1,0:T(8,128)(2,1)S(1)}, bf16[8,144,2048]{2,1,0:T(8,128)(2,1)}) fusion(f32[144,2048]{1,0:T(8,128)S(1)} %copy-done.1, f32[8,2048]{1,0:T(8,128)S(1)} %get-tuple-element.513, f32[144,2048]{1,0:T(8,128)} %sub.196, f32[8,2048]{1,0:T(8,128)S(1)} %get-tuple-element.515), kind=kLoop, calls=%fused_computation.8.clone.1 | loop fusion | flops 18874368 | bytes 11927552 | tf_op jit(solution)/shard_map/while/body/convert_element_type | solution.py:69
  313.1 7.9 %gather_fusion.3 = bf16[2048,24]{1,0:T(8,128)(2,1)S(1)} fusion(bf16[24,12288]{0,1:T(8,128)(2,1)} %get-tuple-element.559, s32[2048]{0:T(1024)S(1)} %broadcast_clamp_fusion.5), kind=kCustom, calls=%fused_computation.1.clone.1 | custom fusion | bytes 204800 | tf_op jit(solution)/shard_map/while/body/jit(_take)/gather | solution.py:56
  328.1 4.4 %subtract_reduce_fusion.2 = (f32[2048]{0:T(1024)S(1)}, f32[2048]{0:T(1024)S(1)}) fusion(f32[144,2048]{1,0:T(8,128)} %add.543, f32[144,2048]{1,0:T(8,128)} %sub.195, f32[144,2048]{1,0:T(8,128)S(1)} %copy-done.2, bf16[144,1152]{1,0:T(8,128)(2,1)S(1)} %copy-done.6, bf16[1152,2048]{1,0:T(8,128)(2,1)} %bitcast.164), kind=kOutput, calls=%fused_computation.17.clone.1 | convolution fusion | flops 681832448 | bytes 8605696 | tf_op jit(solution)/shard_map/while/body/dot_general | solution.py:72
  332.6 38.2 %gather_fusion.1 = bf16[6144]{0:T(1024)(128)(2,1)S(1)} fusion(bf16[49152]{0:T(1024)(128)(2,1)S(1)} %get-tuple-element.564, s32[6144]{0:T(1024)S(1)} %broadcast_clamp_fusion.4), kind=kCustom, calls=%fused_computation.4.clone.1 | custom fusion | bytes 49152 | tf_op jit(solution)/shard_map/while/body/jit(_take)/gather | solution.py:60
  370.8 13.1 %gather_fusion.4 = bf16[2048]{0:T(1024)(128)(2,1)S(1)} fusion(bf16[12288]{0:T(1024)(128)(2,1)S(1)} %get-tuple-element.563, s32[2048]{0:T(1024)S(1)} %broadcast_clamp_fusion.5), kind=kCustom, calls=%fused_computation.3.clone.1 | custom fusion | bytes 16384 | tf_op jit(solution)/shard_map/while/body/jit(_take)/gather | solution.py:57
  384.0 14.7 %scatter_fusion = f32[12288]{0:T(1024)S(1)} fusion(f32[12288]{0:T(1024)S(1)} %get-tuple-element.538, s32[2048]{0:T(1024)S(1)} %bitcast.168, f32[2048]{0:T(1024)S(1)} %fusion.61), kind=kCustom, calls=%fused_computation.5.clone.1 | custom fusion | flops 2048 | bytes 32768 | tf_op jit(solution)/shard_map/while/body/scatter-add | solution.py:134
  398.7 26.3 %all-reduce = f32[12288]{0:T(1024)S(1)} all-reduce(f32[12288]{0:T(1024)S(1)} %get-tuple-element.210), channel_id=2, replica_groups=mesh['pb'=4,'wa'=8] {'wa'}, use_global_device_ids=true, to_apply=%region_8.9.clone | all-reduce | flops 12288 | bytes 98304
  (150 shorter events, 51.4 us)
Async XLA Ops:
  6.5 127.8 %all-gather.2.cloned.1.call-start = ((), (), s32[]{:S(2)}) async-start(), calls=%async_computation.2 | async-start | bytes 15728640 | tf_op jit(solution)/shard_map/all_gather | solution.py:97
  10.3 6.2 %copy-start.9 = (s32[32,4,128]{2,1,0:T(4,128)S(1)}, s32[32,4,128]{2,1,0:T(4,128)}, u32[]{:S(2)}) copy-start(s32[32,4,128]{2,1,0:T(4,128)} %param.8) | copy-start | bytes 196612
  10.3 6.8 %copy-start.13 = (s32[8,9]{1,0:T(8,128)S(1)}, s32[8,9]{1,0:T(8,128)}, u32[]{:S(2)}) copy-start(s32[8,9]{1,0:T(8,128)} %param.13) | copy-start | bytes 868
  10.3 6.9 %copy-start.14 = (u32[32]{0:T(128)S(1)}, u32[32]{0:T(128)}, u32[]{:S(2)}) copy-start(u32[32]{0:T(128)} %constant.294) | copy-start | bytes 388
  10.3 7.5 %copy-start = (bf16[12288]{0:T(1024)(128)(2,1)S(1)}, bf16[12288]{0:T(1024)(128)(2,1)}, u32[]{:S(2)}) copy-start(bf16[12288]{0:T(1024)(128)(2,1)} %param.11) | copy-start | bytes 73732
  11.6 15.7 %all-to-all-start = ((s32[1,8,1]{2,0,1:T(1,128)}), s32[1,8,1]{2,0,1:T(1,128)S(1)}, u32[]{:S(2)}, u32[]{:S(2)}) async-start(s32[1,8,1]{2,0,1:T(1,128)} %broadcast_in_dim.123), calls=%async_computation | async-start | bytes 8192 | tf_op jit(solution)/shard_map/all_to_all | solution.py:105
  27.3 11.0 %all-to-all-start.1 = ((s32[4,8,4,128]{3,2,0,1:T(4,128)}), s32[4,8,4,128]{3,2,0,1:T(4,128)S(1)}, u32[]{:S(2)}, u32[]{:S(2)}) async-start(s32[4,8,4,128]{3,2,0,1:T(4,128)} %copy.94), calls=%async_computation.1 | async-start | bytes 131072 | tf_op jit(solution)/shard_map/all_to_all | solution.py:104
  134.3 2.0 copy-start.11
  134.3 2.0 copy-start.7
  169.8 1.8 copy-start.1
  171.6 5.2 %copy-start.5 = (bf16[144,1152]{1,0:T(8,128)(2,1)S(1)}, bf16[144,1152]{1,0:T(8,128)(2,1)}, u32[]{:S(2)}) copy-start(bf16[144,1152]{1,0:T(8,128)(2,1)} %get-tuple-element.562) | copy-start | bytes 995332 | tf_op jit(solution)/shard_map/while
  176.7 2.0 copy-start.4
  194.2 1.8 copy-start.6
  238.6 13.1 %copy-start.10 = (pred[16]{0:T(512)(128)(4,1)S(1)}, pred[16]{0:T(512)(128)(4,1)}, u32[]{:S(2)}) copy-start(pred[16]{0:T(512)(128)(4,1)} %get-tuple-element.520) | copy-start | bytes 52 | tf_op jit(solution)/shard_map/while
  251.8 14.7 %copy-start.8 = (s32[32,4,128]{2,1,0:T(4,128)S(1)}, s32[32,4,128]{2,1,0:T(4,128)}, u32[]{:S(2)}) copy-start(s32[32,4,128]{2,1,0:T(4,128)} %copy-done.7) | copy-start | bytes 196612 | tf_op jit(solution)/shard_map/while
  251.8 14.7 %copy-start.12 = (s32[32]{0:T(128)S(1)}, s32[32]{0:T(128)}, u32[]{:S(2)}) copy-start(s32[32]{0:T(128)} %copy-done.11) | copy-start | bytes 388 | tf_op jit(solution)/shard_map/while
  266.5 2.0 copy-start.11
  266.5 2.0 copy-start.7
  302.0 1.8 copy-start.1
  303.8 5.2 %copy-start.5 = (bf16[144,1152]{1,0:T(8,128)(2,1)S(1)}, bf16[144,1152]{1,0:T(8,128)(2,1)}, u32[]{:S(2)}) copy-start(bf16[144,1152]{1,0:T(8,128)(2,1)} %get-tuple-element.562) | copy-start | bytes 995332 | tf_op jit(solution)/shard_map/while
  308.9 2.0 copy-start.4
  370.8 13.1 %copy-start.10 = (pred[16]{0:T(512)(128)(4,1)S(1)}, pred[16]{0:T(512)(128)(4,1)}, u32[]{:S(2)}) copy-start(pred[16]{0:T(512)(128)(4,1)} %get-tuple-element.520) | copy-start | bytes 52 | tf_op jit(solution)/shard_map/while
  384.0 14.7 %copy-start.8 = (s32[32,4,128]{2,1,0:T(4,128)S(1)}, s32[32,4,128]{2,1,0:T(4,128)}, u32[]{:S(2)}) copy-start(s32[32,4,128]{2,1,0:T(4,128)} %copy-done.7) | copy-start | bytes 196612 | tf_op jit(solution)/shard_map/while
  384.0 14.7 %copy-start.12 = (s32[32]{0:T(128)S(1)}, s32[32]{0:T(128)}, u32[]{:S(2)}) copy-start(s32[32]{0:T(128)} %copy-done.11) | copy-start | bytes 388 | tf_op jit(solution)/shard_map/while
  (5 other events, 7.6 us)
Sparse Core Ops, SparseCore 0:
  10.4 123.8 all-gather.1
where the time goes:
time: 433 us
  local copies, waits for them, and re-layouts  206 us (48%)
  waiting for transfers between devices  99.1 us (23%)
  other arithmetic  53.5 us (12%)
  blocking collectives  35.3 us (8%)
  between operations  15.4 us (4%)
  matrix products  12.8 us (3%)
  starting transfers between devices  9.98 us (2%)
    all_gather x1, waiting for transfers between devices, body(): lax.all_gather(eig, 'pb', axis=1, tiled=True)  95.9 us
    gather x2, local copies, waits for them, and re-layouts, contributions(): jnp.take(frequencies, flat_spots).astype(jnp.float32).reshape(3, count)  76.4 us
    gather x2, local copies, waits for them, and re-layouts, contributions(): gathered = jnp.take(vectors, flat_spots, axis=1).astype(jnp.float32)  45.3 us
    scatter-add x2, other arithmetic, one_round(): return partial_value.at[first_modes].add(terms)  29.4 us
    unnamed x1, blocking collectives  26.3 us
    gather x2, local copies, waits for them, and re-layouts, contributions(): first_freq = jnp.take(first_freqs, first_modes).astype(jnp.float32)  26.2 us
    gather x2, local copies, waits for them, and re-layouts, contributions(): first_vec = jnp.take(first_vectors, first_modes, axis=1).astype(jnp.float32)  15.8 us
    convert_element_type x2, other arithmetic, contributions(): wide_re.reshape(clusters * branches * branches, count).astype(jnp.bfloat16)  10.3 us
  transfers between devices with their start and end apart: 3, of which 2 were waited for; matrix products, arithmetic and copies ran while one was open for 1% of the time, Pallas kernels for 0%

commit v1 on v0

--- a/solution.py
+++ b/solution.py
@@ -3,6 +3,7 @@
 import jax.numpy as jnp
 from jax import lax
 from jax.sharding import PartitionSpec as P
+from jax.lax import all_gather
 
 QMESH = 16
 smearing = 0.5
@@ -93,10 +94,11 @@
     held = quartets.shape[0]
     block = quartets.shape[2]
     group = math.gcd(held, 16)
-    table, freq_table = (
-        lax.all_gather(eig, "pb", axis=1, tiled=True),
-        lax.all_gather(freq, "pb", axis=0, tiled=True),
-    )
+
+    def get_targets(frame, dim_no):
+        return jnp.concatenate(all_gather(frame, "pb"), axis=dim_no)
+
+    table, freq_table = (get_targets(eig, 1), lax.all_gather(freq, "pb", axis=0, tiled=True))
     per_dest = held // workers
     dealt = quartets.reshape(per_dest, workers, 4, block)
     tallies = jnp.full((1, workers), counts[0], jnp.int32)

time: 433 us -> 358 us (0.83)
  waiting for transfers between devices: 99.1 us -> 13.4 us
  local copies, waits for them, and re-layouts: 206 us -> 216 us
    all_gather x1, waiting for transfers between devices: 95.9 us -> 9.55 us  [get_targets(): return jnp.concatenate(all_gather(frame, 'pb'), axis=dim_no)]
    all_gather x0 -> x1, local copies, waits for them, and re-layouts: none -> 10.1 us  [get_targets(): return jnp.concatenate(all_gather(frame, 'pb'), axis=dim_no)]
  transfers between devices with their start and end apart: 3 -> 3, of which waited for: 2 -> 2; matrix products, arithmetic and copies ran while one was open for 1% -> 2% of each run, Pallas kernels for 0% -> 0%
where the time goes in v1:
time: 358 us; the launch traced here: 357 us
  local copies, waits for them, and re-layouts  216 us (60%)
  other arithmetic  53.6 us (15%)
  blocking collectives  35.3 us (10%)
  between operations  15.4 us (4%)
  waiting for transfers between devices  13.4 us (4%)
  matrix products  12.8 us (4%)
  starting transfers between devices  9.71 us (3%)
    gather x2, local copies, waits for them, and re-layouts, contributions(): jnp.take(frequencies, flat_spots).astype(jnp.float32).reshape(3, count)  76.4 us
    gather x2, local copies, waits for them, and re-layouts, contributions(): gathered = jnp.take(vectors, flat_spots, axis=1).astype(jnp.float32)  45.3 us
    scatter-add x2, other arithmetic, one_round(): return partial_value.at[first_modes].add(terms)  29.4 us
    unnamed x1, blocking collectives  26.3 us
    gather x2, local copies, waits for them, and re-layouts, contributions(): first_freq = jnp.take(first_freqs, first_modes).astype(jnp.float32)  26.2 us
    gather x2, local copies, waits for them, and re-layouts, contributions(): first_vec = jnp.take(first_vectors, first_modes, axis=1).astype(jnp.float32)  15.8 us
    convert_element_type x2, other arithmetic, contributions(): wide_re.reshape(clusters * branches * branches, count).astype(jnp.bfloat16)  10.3 us
    all_gather x1, local copies, waits for them, and re-layouts, get_targets(): return jnp.concatenate(all_gather(frame, 'pb'), axis=dim_no)  10.1 us
  transfers between devices with their start and end apart: 3, of which 2 were waited for; matrix products, arithmetic and copies ran while one was open for 2% of the time, Pallas kernels for 0%

profile of v1, /device:TPU:4, one launch (start us, length us, event | category | flops | bytes accessed | tf_op | source)
XLA Modules:
  0.0 356.9 jit_solution(12447963979101739622)
XLA Ops:
  8.5 4.9 %all-to-all-start = ((s32[1,8,1]{2,0,1:T(1,128)}), s32[1,8,1]{2,0,1:T(1,128)S(1)}, u32[]{:S(2)}, u32[]{:S(2)}) async-start(s32[1,8,1]{2,0,1:T(1,128)} %broadcast_in_dim.123), calls=%async_computation | async-start | bytes 8192 | tf_op jit(solution)/shard_map/all_to_all | solution.py:107
  13.4 3.8 %copy.98 = bf16[24,12288]{0,1:T(8,128)(2,1)} copy(bf16[24,12288]{1,0:T(8,128)(2,1)} %param.10) | data formatting | bytes 1179648 | tf_op jit(solution)/shard_map/while | solution.py:138
  18.5 9.0 %all_gather.11 = bf16[49152]{0:T(1024)(128)(2,1)S(1)} all-gather(bf16[12288]{0:T(1024)(128)(2,1)S(1)} %copy-done), channel_id=1, replica_groups=mesh['pb'=4,'wa'=8] {'pb'}, dimensions={0}, use_global_device_ids=true | all-gather | bytes 122880 | tf_op jit(solution)/shard_map/all_gather | solution.py:101
  28.2 4.8 %all-to-all-start.1 = ((s32[4,8,4,128]{3,2,0,1:T(4,128)}), s32[4,8,4,128]{3,2,0,1:T(4,128)S(1)}, u32[]{:S(2)}, u32[]{:S(2)}) async-start(s32[4,8,4,128]{3,2,0,1:T(4,128)} %copy.94), calls=%async_computation.1 | async-start | bytes 131072 | tf_op jit(solution)/shard_map/all_to_all | solution.py:106
  35.8 3.2 all-to-all-done.1
  39.0 9.6 %all-gather.3.cloned.1.call-done = bf16[96,12288]{1,0:T(8,128)(2,1)} async-done(((bf16[24,12288]{1,0:T(8,128)(2,1)}), bf16[96,12288]{1,0:T(8,128)(2,1)}) %all-gather.3.cloned.1.call-update) | async-done | bytes 2359312 | tf_op jit(solution)/shard_map/all_gather | solution.py:99
  48.6 10.1 %copy.96 = bf16[4,24,12288]{1,2,0:T(8,128)(2,1)} copy(bf16[4,24,12288]{2,1,0:T(8,128)(2,1)} %bitcast.172) | data formatting | bytes 4718592 | tf_op jit(solution)/shard_map/all_gather | solution.py:99
  58.6 264.4 %while.13 = (s32[]{:T(128)}, f32[12288]{0:T(1024)S(1)}, s32[]{:T(128)}, s32[32]{0:T(128)S(1)}, s32[32,4,128]{2,1,0:T(4,128)S(1)}, /*index=5*/s32[]{:T(128)}, bf1...) while((s32[]{:T(128)}, f32[12288]{0:T(1024)S(1)}, ...), condition=%wide.region_7.8_spmd, body=%wide.region_3.7_spmd.sunk | while | flops 1385344256 | bytes 61334244 | solution.py:138
  60.6 22.7 %gather_fusion.2 = bf16[6144,24]{1,0:T(8,128)(2,1)S(1)} fusion(bf16[24,49152]{0,1:T(8,128)(2,1)} %get-tuple-element.560, s32[6144]{0:T(1024)S(1)} %broadcast_clamp_fusion.4), kind=kCustom, calls=%fused_computation.2.clone.1 | custom fusion | bytes 614400 | tf_op jit(solution)/shard_map/while/body/jit(_take)/gather | solution.py:60
  84.4 2.5 fusion.55
  95.9 5.2 %subtract_convert_fusion.2 = (bf16[8,144,2048]{2,1,0:T(8,128)(2,1)S(1)}, bf16[8,144,2048]{2,1,0:T(8,128)(2,1)}) fusion(f32[144,2048]{1,0:T(8,128)S(1)} %copy-done.1, f32[8,2048]{1,0:T(8,128)S(1)} %get-tuple-element.513, f32[144,2048]{1,0:T(8,128)} %sub.196, f32[8,2048]{1,0:T(8,128)S(1)} %get-tuple-element.515), kind=kLoop, calls=%fused_computation.8.clone.1 | loop fusion | flops 18874368 | bytes 11927552 | tf_op jit(solution)/shard_map/while/body/convert_element_type | solution.py:70
  105.3 7.9 %gather_fusion.3 = bf16[2048,24]{1,0:T(8,128)(2,1)S(1)} fusion(bf16[24,12288]{0,1:T(8,128)(2,1)} %get-tuple-element.559, s32[2048]{0:T(1024)S(1)} %broadcast_clamp_fusion.5), kind=kCustom, calls=%fused_computation.1.clone.1 | custom fusion | bytes 204800 | tf_op jit(solution)/shard_map/while/body/jit(_take)/gather | solution.py:57
  120.2 4.4 %subtract_reduce_fusion.2 = (f32[2048]{0:T(1024)S(1)}, f32[2048]{0:T(1024)S(1)}) fusion(f32[144,2048]{1,0:T(8,128)} %add.543, f32[144,2048]{1,0:T(8,128)} %sub.195, f32[144,2048]{1,0:T(8,128)S(1)} %copy-done.2, bf16[144,1152]{1,0:T(8,128)(2,1)S(1)} %copy-done.6, bf16[1152,2048]{1,0:T(8,128)(2,1)} %bitcast.168), kind=kOutput, calls=%fused_computation.17.clone.1 | convolution fusion | flops 681832448 | bytes 8605696 | tf_op jit(solution)/shard_map/while/body/dot_general | solution.py:73
  124.7 38.2 %gather_fusion.1 = bf16[6144]{0:T(1024)(128)(2,1)S(1)} fusion(bf16[49152]{0:T(1024)(128)(2,1)S(1)} %get-tuple-element.564, s32[6144]{0:T(1024)S(1)} %broadcast_clamp_fusion.4), kind=kCustom, calls=%fused_computation.4.clone.1 | custom fusion | bytes 49152 | tf_op jit(solution)/shard_map/while/body/jit(_take)/gather | solution.py:61
  162.9 13.1 %gather_fusion.4 = bf16[2048]{0:T(1024)(128)(2,1)S(1)} fusion(bf16[12288]{0:T(1024)(128)(2,1)S(1)} %get-tuple-element.563, s32[2048]{0:T(1024)S(1)} %broadcast_clamp_fusion.5), kind=kCustom, calls=%fused_computation.3.clone.1 | custom fusion | bytes 16384 | tf_op jit(solution)/shard_map/while/body/jit(_take)/gather | solution.py:58
  176.1 14.7 %scatter_fusion = f32[12288]{0:T(1024)S(1)} fusion(f32[12288]{0:T(1024)S(1)} %get-tuple-element.538, s32[2048]{0:T(1024)S(1)} %bitcast.174, f32[2048]{0:T(1024)S(1)} %fusion.61), kind=kCustom, calls=%fused_computation.5.clone.1 | custom fusion | flops 2048 | bytes 32768 | tf_op jit(solution)/shard_map/while/body/scatter-add | solution.py:136
  192.8 22.6 %gather_fusion.2 = bf16[6144,24]{1,0:T(8,128)(2,1)S(1)} fusion(bf16[24,49152]{0,1:T(8,128)(2,1)} %get-tuple-element.560, s32[6144]{0:T(1024)S(1)} %broadcast_clamp_fusion.4), kind=kCustom, calls=%fused_computation.2.clone.1 | custom fusion | bytes 614400 | tf_op jit(solution)/shard_map/while/body/jit(_take)/gather | solution.py:60
  228.1 5.2 %subtract_convert_fusion.2 = (bf16[8,144,2048]{2,1,0:T(8,128)(2,1)S(1)}, bf16[8,144,2048]{2,1,0:T(8,128)(2,1)}) fusion(f32[144,2048]{1,0:T(8,128)S(1)} %copy-done.1, f32[8,2048]{1,0:T(8,128)S(1)} %get-tuple-element.513, f32[144,2048]{1,0:T(8,128)} %sub.196, f32[8,2048]{1,0:T(8,128)S(1)} %get-tuple-element.515), kind=kLoop, calls=%fused_computation.8.clone.1 | loop fusion | flops 18874368 | bytes 11927552 | tf_op jit(solution)/shard_map/while/body/convert_element_type | solution.py:70
  237.5 7.9 %gather_fusion.3 = bf16[2048,24]{1,0:T(8,128)(2,1)S(1)} fusion(bf16[24,12288]{0,1:T(8,128)(2,1)} %get-tuple-element.559, s32[2048]{0:T(1024)S(1)} %broadcast_clamp_fusion.5), kind=kCustom, calls=%fused_computation.1.clone.1 | custom fusion | bytes 204800 | tf_op jit(solution)/shard_map/while/body/jit(_take)/gather | solution.py:57
  252.4 4.4 %subtract_reduce_fusion.2 = (f32[2048]{0:T(1024)S(1)}, f32[2048]{0:T(1024)S(1)}) fusion(f32[144,2048]{1,0:T(8,128)} %add.543, f32[144,2048]{1,0:T(8,128)} %sub.195, f32[144,2048]{1,0:T(8,128)S(1)} %copy-done.2, bf16[144,1152]{1,0:T(8,128)(2,1)S(1)} %copy-done.6, bf16[1152,2048]{1,0:T(8,128)(2,1)} %bitcast.168), kind=kOutput, calls=%fused_computation.17.clone.1 | convolution fusion | flops 681832448 | bytes 8605696 | tf_op jit(solution)/shard_map/while/body/dot_general | solution.py:73
  256.9 38.2 %gather_fusion.1 = bf16[6144]{0:T(1024)(128)(2,1)S(1)} fusion(bf16[49152]{0:T(1024)(128)(2,1)S(1)} %get-tuple-element.564, s32[6144]{0:T(1024)S(1)} %broadcast_clamp_fusion.4), kind=kCustom, calls=%fused_computation.4.clone.1 | custom fusion | bytes 49152 | tf_op jit(solution)/shard_map/while/body/jit(_take)/gather | solution.py:61
  295.1 13.1 %gather_fusion.4 = bf16[2048]{0:T(1024)(128)(2,1)S(1)} fusion(bf16[12288]{0:T(1024)(128)(2,1)S(1)} %get-tuple-element.563, s32[2048]{0:T(1024)S(1)} %broadcast_clamp_fusion.5), kind=kCustom, calls=%fused_computation.3.clone.1 | custom fusion | bytes 16384 | tf_op jit(solution)/shard_map/while/body/jit(_take)/gather | solution.py:58
  308.3 14.7 %scatter_fusion = f32[12288]{0:T(1024)S(1)} fusion(f32[12288]{0:T(1024)S(1)} %get-tuple-element.538, s32[2048]{0:T(1024)S(1)} %bitcast.174, f32[2048]{0:T(1024)S(1)} %fusion.61), kind=kCustom, calls=%fused_computation.5.clone.1 | custom fusion | flops 2048 | bytes 32768 | tf_op jit(solution)/shard_map/while/body/scatter-add | solution.py:136
  323.0 26.3 %all-reduce = f32[12288]{0:T(1024)S(1)} all-reduce(f32[12288]{0:T(1024)S(1)} %get-tuple-element.210), channel_id=3, replica_groups=mesh['pb'=4,'wa'=8] {'wa'}, use_global_device_ids=true, to_apply=%region_8.9.clone | all-reduce | flops 12288 | bytes 98304
  (151 shorter events, 54.6 us)
Async XLA Ops:
  6.5 42.0 %all-gather.3.cloned.1.call-start = ((), (), s32[]{:S(2)}) async-start(), calls=%async_computation.2 | async-start | bytes 2949120 | tf_op jit(solution)/shard_map/all_gather | solution.py:99
  8.5 19.7 %all-to-all-start = ((s32[1,8,1]{2,0,1:T(1,128)}), s32[1,8,1]{2,0,1:T(1,128)S(1)}, u32[]{:S(2)}, u32[]{:S(2)}) async-start(s32[1,8,1]{2,0,1:T(1,128)} %broadcast_in_dim.123), calls=%async_computation | async-start | bytes 8192 | tf_op jit(solution)/shard_map/all_to_all | solution.py:107
  13.4 3.8 %copy-start.9 = (s32[32,4,128]{2,1,0:T(4,128)S(1)}, s32[32,4,128]{2,1,0:T(4,128)}, u32[]{:S(2)}) copy-start(s32[32,4,128]{2,1,0:T(4,128)} %param.8) | copy-start | bytes 196612
  13.4 4.5 %copy-start.13 = (s32[8,9]{1,0:T(8,128)S(1)}, s32[8,9]{1,0:T(8,128)}, u32[]{:S(2)}) copy-start(s32[8,9]{1,0:T(8,128)} %param.13) | copy-start | bytes 868
  13.4 4.5 %copy-start.14 = (u32[32]{0:T(128)S(1)}, u32[32]{0:T(128)}, u32[]{:S(2)}) copy-start(u32[32]{0:T(128)} %constant.294) | copy-start | bytes 388
  13.4 5.1 %copy-start = (bf16[12288]{0:T(1024)(128)(2,1)S(1)}, bf16[12288]{0:T(1024)(128)(2,1)}, u32[]{:S(2)}) copy-start(bf16[12288]{0:T(1024)(128)(2,1)} %param.11) | copy-start | bytes 73732
  28.2 10.7 %all-to-all-start.1 = ((s32[4,8,4,128]{3,2,0,1:T(4,128)}), s32[4,8,4,128]{3,2,0,1:T(4,128)S(1)}, u32[]{:S(2)}, u32[]{:S(2)}) async-start(s32[4,8,4,128]{3,2,0,1:T(4,128)} %copy.94), calls=%async_computation.1 | async-start | bytes 131072 | tf_op jit(solution)/shard_map/all_to_all | solution.py:106
  58.6 2.0 copy-start.7
  94.1 1.8 copy-start.1
  95.9 5.2 %copy-start.5 = (bf16[144,1152]{1,0:T(8,128)(2,1)S(1)}, bf16[144,1152]{1,0:T(8,128)(2,1)}, u32[]{:S(2)}) copy-start(bf16[144,1152]{1,0:T(8,128)(2,1)} %get-tuple-element.562) | copy-start | bytes 995332 | tf_op jit(solution)/shard_map/while
  101.1 2.0 copy-start.4
  118.5 1.7 copy-start.2
  118.5 1.8 copy-start.6
  162.9 13.1 %copy-start.10 = (pred[16]{0:T(512)(128)(4,1)S(1)}, pred[16]{0:T(512)(128)(4,1)}, u32[]{:S(2)}) copy-start(pred[16]{0:T(512)(128)(4,1)} %get-tuple-element.520) | copy-start | bytes 52 | tf_op jit(solution)/shard_map/while
  176.1 14.7 %copy-start.8 = (s32[32,4,128]{2,1,0:T(4,128)S(1)}, s32[32,4,128]{2,1,0:T(4,128)}, u32[]{:S(2)}) copy-start(s32[32,4,128]{2,1,0:T(4,128)} %copy-done.7) | copy-start | bytes 196612 | tf_op jit(solution)/shard_map/while
  176.1 14.7 %copy-start.12 = (s32[32]{0:T(128)S(1)}, s32[32]{0:T(128)}, u32[]{:S(2)}) copy-start(s32[32]{0:T(128)} %copy-done.11) | copy-start | bytes 388 | tf_op jit(solution)/shard_map/while
  190.8 2.0 copy-start.7
  226.3 1.8 copy-start.1
  228.1 5.2 %copy-start.5 = (bf16[144,1152]{1,0:T(8,128)(2,1)S(1)}, bf16[144,1152]{1,0:T(8,128)(2,1)}, u32[]{:S(2)}) copy-start(bf16[144,1152]{1,0:T(8,128)(2,1)} %get-tuple-element.562) | copy-start | bytes 995332 | tf_op jit(solution)/shard_map/while
  233.3 2.0 copy-start.4
  250.7 1.8 copy-start.6
  295.1 13.1 %copy-start.10 = (pred[16]{0:T(512)(128)(4,1)S(1)}, pred[16]{0:T(512)(128)(4,1)}, u32[]{:S(2)}) copy-start(pred[16]{0:T(512)(128)(4,1)} %get-tuple-element.520) | copy-start | bytes 52 | tf_op jit(solution)/shard_map/while
  308.3 14.7 %copy-start.8 = (s32[32,4,128]{2,1,0:T(4,128)S(1)}, s32[32,4,128]{2,1,0:T(4,128)}, u32[]{:S(2)}) copy-start(s32[32,4,128]{2,1,0:T(4,128)} %copy-done.7) | copy-start | bytes 196612 | tf_op jit(solution)/shard_map/while
  308.3 14.7 %copy-start.12 = (s32[32]{0:T(128)S(1)}, s32[32]{0:T(128)}, u32[]{:S(2)}) copy-start(s32[32]{0:T(128)} %copy-done.11) | copy-start | bytes 388 | tf_op jit(solution)/shard_map/while
  (5 other events, 6.7 us)
Sparse Core Ops, SparseCore 0:
  9.2 39.3 all-gather.2
